TPU v7x, 32 devices: a whole 2x2x4 slice. The times are simulated.
32 devices in a mesh: blk: 8 (over z, x), dp: 4 (over y, core).
Axes of the slice: x: 2, y: 2, z: 4, core: 2. Of those that a mesh axis runs over, the one named last changes fastest.
Arguments:
- tokens: bfloat16 [1024, 5120], P('blk', 'dp'), may hold values from -6 to 6
- expert_ids: int32 [1024, 6], P('blk'), may hold values from 0 to 15, all different within a row; in each aligned block of 128 rows (0 to 127, 128 to 255, ...) at most 96 rows name the same one
- gate_vals: float32 [1024, 6], P('blk'), may hold values from 0.1 to 1
- w_gate: bfloat16 [16, 5120, 1536], P('blk', 'dp'), may hold values from -0.078125 to 0.078125
- w_up: bfloat16 [16, 5120, 1536], P('blk', 'dp'), may hold values from -0.078125 to 0.078125
- w_down: bfloat16 [16, 5120, 1536], P('blk', 'dp'), may hold values from -0.15625 to 0.15625
Outputs:
- combined: bfloat16 [1024, 5120], P('blk', 'dp')
Inputs may be any that keep to these rules, and one draw needn't show every extreme that they name: `expert_ids`: each row names 6 different experts. Among the 128 rows of one index of blk (aligned blocks) no expert is named more than 96 times, a bound that some block reaches.
All inputs are finite; a program needn't handle non-finite values.
Results may differ from a plain program's by a relative error of at most 0.0057.
Values may be sent and summed in bfloat16 or wider, within the bound.
A program may use at most 128 MiB of HBM per device.

v0:
```python
import jax
import jax.numpy as jnp
from jax import lax
from jax.sharding import PartitionSpec as P


def local(tokens, expert_ids, gate_vals, w_gate, w_up, w_down):
    blk_size = lax.axis_size("blk")
    tok_rows, width_dev = tokens.shape
    top_k = expert_ids.shape[1]
    held_count = w_gate.shape[0]
    n_total = held_count * blk_size
    capacity = 2 * tok_rows * top_k // n_total
    flat_ids = expert_ids.reshape(-1)
    onehot = (flat_ids[:, None] == jnp.arange(n_total, dtype=jnp.int32)[None, :]).astype(jnp.int32)
    before = jnp.cumsum(onehot, axis=0) - onehot
    position = jnp.sum(before * onehot, axis=1)
    owner_blk = flat_ids // held_count
    within = flat_ids % held_count
    slot_index = (owner_blk * capacity + position) * held_count + within
    copies = jnp.repeat(tokens, top_k, axis=0)
    buffer = (
        jnp.zeros((blk_size * capacity * held_count, width_dev), jnp.bfloat16)
        .at[slot_index]
        .set(copies)
    )
    buffer = buffer.reshape(blk_size, capacity, held_count, width_dev)
    arrived = lax.all_to_all(buffer, "blk", split_axis=0, concat_axis=0, tiled=True)
    row_count = blk_size * capacity
    arrived = arrived.reshape(row_count, held_count, width_dev)
    gate_part = jnp.einsum("med,edf->mef", arrived, w_gate, preferred_element_type=jnp.float32)
    up_part = jnp.einsum("med,edf->mef", arrived, w_up, preferred_element_type=jnp.float32)
    summed = lax.psum_scatter(
        jnp.stack((gate_part, up_part), axis=2), "dp", scatter_dimension=3, tiled=True
    )
    hidden = (jax.nn.silu(summed[:, :, 0]) * summed[:, :, 1]).astype(jnp.bfloat16)
    result = jnp.einsum(
        "mef,edf->med",
        lax.all_gather(hidden, "dp", axis=2, tiled=True),
        w_down,
        preferred_element_type=jnp.float32,
    )
    outgoing = result.astype(jnp.bfloat16).reshape(blk_size, capacity, held_count, width_dev)
    returned = lax.all_to_all(outgoing, "blk", split_axis=0, concat_axis=0, tiled=True).reshape(
        -1, width_dev
    )
    picked = returned[slot_index].astype(jnp.float32).reshape(tok_rows, top_k, width_dev)
    combined = jnp.sum(picked * gate_vals[:, :, None], axis=1)
    return combined.astype(jnp.bfloat16)


def solution(mesh):
    return jax.shard_map(
        local,
        mesh=mesh,
        in_specs=(
            P("blk", "dp"),
            P("blk", None),
            P("blk", None),
            P("blk", "dp", None),
            P("blk", "dp", None),
            P("blk", "dp", None),
        ),
        out_specs=P("blk", "dp"),
        check_vma=False,
    )
```

profile of v0, /device:TPU:0, one launch (start us, length us, event | category | flops | bytes accessed | tf_op | source)
XLA Modules:
  0.0 473.4 jit_solution(6178207520856967586)
XLA Ops:
  6.5 0.0 reduce-scatter.2.cloned.1.call-start
  6.5 0.8 copy.16
  7.3 0.1 eq.31
  7.5 0.1 eq.27
  7.6 0.1 reshape.160
  7.8 1.7 reduce-window.6
  9.5 0.3 slice_reduce_fusion
  9.8 1.3 broadcast_in_dim.5
  11.0 2.1 reshape.180
  13.2 0.1 fusion.6
  13.3 9.1 %scatter_custom_fusion = bf16[1536,1280]{1,0:T(8,128)(2,1)} fusion(s32[768]{0:T(1024)S(1)} %fusion.9, bf16[768,1280]{1,0:T(8,128)(2,1)} %reshape.180, bf16[]{:T(256)} %constant.35.clone.1), kind=kCustom, calls=%fused_computation.11 | custom fusion | bytes 3932672 | tf_op jit(solution)/shard_map/scatter | solution.py:25
  22.4 8.7 %reshape.163 = bf16[8,96,2,1280]{3,2,1,0:T(2,128)(2,1)} reshape(bf16[1536,1280]{1,0:T(8,128)(2,1)} %scatter_custom_fusion) | data formatting | bytes 7864320 | tf_op jit(solution)/shard_map/reshape | solution.py:27
  31.1 0.0 slice-start
  31.1 95.1 %all_to_all.10 = bf16[8,96,2,1280]{3,2,1,0:T(2,128)(2,1)S(1)} all-to-all(bf16[8,96,2,1280]{3,2,1,0:T(2,128)(2,1)} %reshape.163), channel_id=1, replica_groups=mesh['blk'=8,'dp'=4] {'blk'}, dimensions={0} | all-to-all | bytes 7864320 | tf_op jit(solution)/shard_map/all_to_all | solution.py:28
  126.2 0.0 slice-start.1
  126.2 0.6 copy.20
  126.8 0.0 slice-done
  126.8 1.4 slice-done.1
  128.2 6.2 %convolution_bitcast_fusion = f32[768,2,1,1536]{3,0,1,2:T(8,128)S(1)} fusion(bf16[768,2,1280]{2,0,1:T(8,128)(2,1)S(1)} %bitcast.48, bf16[2,1280,1536]{2,1,0:T(8,128)(2,1)S(1)} %bitcast.53), kind=kOutput, calls=%fused_computation.3 | convolution fusion | flops 6039797760 | bytes 21233664 | tf_op jit(solution)/shard_map/med,edf->mef/dot_general | solution.py:32
  134.5 8.5 %convolution_bitcast_fusion.1 = f32[768,2,1,1536]{3,0,1,2:T(8,128)S(1)} fusion(bf16[768,2,1280]{2,0,1:T(8,128)(2,1)S(1)} %bitcast.49, bf16[2,1280,1536]{2,1,0:T(8,128)(2,1)} %param.9), kind=kOutput, calls=%fused_computation.4 | convolution fusion | flops 6039797760 | bytes 21233664 | tf_op jit(solution)/shard_map/med,edf->mef/dot_general | solution.py:31
  143.0 6.8 %pad_maximum_fusion = f32[768,2,2,1536]{3,0,1,2:T(8,128)} fusion(f32[768,2,1,1536]{3,0,1,2:T(8,128)S(1)} %convolution_bitcast_fusion, f32[768,2,1,1536]{3,0,1,2:T(8,128)S(1)} %convolution_bitcast_fusion.1), kind=kLoop, calls=%fused_computation.2 | loop fusion | flops 4718592 | bytes 37748736 | tf_op jit(solution)/shard_map/stack | solution.py:34
  149.8 0.0 reduce-scatter.2.cloned.1.call-update
  149.8 0.0 all-gather.2.cloned.1.call-start
  149.9 136.8 %reduce-scatter.2.cloned.1.call-done = f32[768,2,2,384]{3,0,1,2:T(8,128)} async-done(((f32[768,2,2,1536]{3,0,1,2:T(8,128)}), f32[768,2,2,384]{3,0,1,2:T(8,128)}) %reduce-scatter.2.cloned.1.call-update) | async-done | bytes 4718608 | tf_op jit(solution)/shard_map/reduce_scatter | solution.py:33
  286.7 4.1 fusion.1
  290.8 0.0 all-gather.2.cloned.1.call-update
  290.8 37.5 %all-gather.2.cloned.1.call-done = bf16[768,2,1536]{2,0,1:T(8,128)(2,1)} async-done(((bf16[768,2,384]{2,0,1:T(8,128)(2,1)}), bf16[768,2,1536]{2,0,1:T(8,128)(2,1)}) %all-gather.2.cloned.1.call-update) | async-done | bytes 4718608 | tf_op jit(solution)/shard_map/all_gather | solution.py:39
  328.3 10.5 %convolution_convert_fusion = bf16[2,768,1280]{2,1,0:T(8,128)(2,1)S(1)} fusion(bf16[768,2,1536]{2,0,1:T(8,128)(2,1)} %all-gather.2.cloned.1.call-done, bf16[2,1280,1536]{2,1,0:T(8,128)(2,1)} %param.11), kind=kOutput, calls=%fused_computation.6 | convolution fusion | flops 6041763840 | bytes 16515072 | tf_op jit(solution)/shard_map/mef,edf->med/dot_general | solution.py:37
  338.8 2.2 copy.21
  341.0 0.0 copy-start
  341.0 5.6 %all-to-all-start.1 = ((bf16[8,96,2,1280]{3,1,2,0:T(8,128)(2,1)}), bf16[8,96,2,1280]{3,1,2,0:T(8,128)(2,1)}, u32[]{:S(2)}, u32[]{:S(2)}) async-start(bf16[8,96,2,1280]{3,1,2,0:T(8,128)(2,1)} %copy.21), calls=%async_computation.2 | async-start | bytes 7864320 | tf_op jit(solution)/shard_map/all_to_all | solution.py:44
  346.6 0.0 copy-done
  346.6 0.1 copy.23
  346.7 87.9 %all-to-all-done.1 = bf16[8,96,2,1280]{3,1,2,0:T(8,128)(2,1)} async-done(((bf16[8,96,2,1280]{3,1,2,0:T(8,128)(2,1)}), bf16[8,96,2,1280]{3,1,2,0:T(8,128)(2,1)}, u32[]{:S(2)}, u32[]{:S(2)}) %all-to-all-start.1) | async-done | bytes 3932192 | tf_op jit(solution)/shard_map/all_to_all | solution.py:44
  434.7 8.1 %copy.22 = bf16[8,96,2,1280]{3,2,1,0:T(2,128)(2,1)} copy(bf16[8,96,2,1280]{3,1,2,0:T(8,128)(2,1)} %all-to-all-done.1) | data formatting | bytes 7864320 | tf_op jit(solution)/shard_map/all_to_all | solution.py:44
  442.7 9.0 %reshape.166 = bf16[1536,1280]{1,0:T(8,128)(2,1)} reshape(bf16[8,96,2,1280]{3,2,1,0:T(2,128)(2,1)} %copy.22) | data formatting | bytes 7864320 | tf_op jit(solution)/shard_map/reshape | solution.py:44
  451.8 7.0 %gather_fusion = bf16[768,1280]{1,0:T(8,128)(2,1)S(1)} fusion(bf16[1536,1280]{1,0:T(8,128)(2,1)} %reshape.166, s32[1024]{0:T(1024)S(1)} %pad_clamp_fusion), kind=kCustom, calls=%fused_computation | custom fusion | bytes 3935232 | tf_op jit(solution)/shard_map/gather | solution.py:47
  458.8 2.9 reshape.167
  461.7 4.9 %multiply_reduce_fusion = bf16[128,1280]{1,0:T(8,128)(2,1)} fusion(f32[128,6,1280]{2,1,0:T(8,128)} %reshape.167, f32[128,6]{1,0:T(8,128)S(1)} %copy.23), kind=kLoop, calls=%fused_computation.5 | loop fusion | flops 1802240 | bytes 4262912 | tf_op jit(solution)/shard_map/reduce_sum | solution.py:48
  (5 shorter events, 0.1 us)
Async XLA Ops:
  6.5 280.2 %reduce-scatter.2.cloned.1.call-start = ((), (), s32[]{:S(2)}) async-start(), calls=%async_computation.3 | async-start | bytes 23592960 | tf_op jit(solution)/shard_map/reduce_scatter | solution.py:33
  31.1 95.7 %slice-start = ((s8[7864320]{0:T(1024)(128)(4,1)}), s8[4194304]{0:T(1024)(128)(4,1)S(1)}, s32[]{:S(2)}) async-start(s8[7864320]{0:T(1024)(128)(4,1)} %bitcast.52), calls=%async_computation.5 | async-start | bytes 8388608
  126.2 2.0 slice-start.1
  149.8 178.5 %all-gather.2.cloned.1.call-start = ((), (), s32[]{:S(2)}) async-start(), calls=%async_computation.4 | async-start | bytes 5898240 | tf_op jit(solution)/shard_map/all_gather | solution.py:39
  341.0 5.6 %copy-start = (f32[128,6]{0,1:T(8,128)S(1)}, f32[128,6]{0,1:T(8,128)}, u32[]{:S(2)}) copy-start(f32[128,6]{0,1:T(8,128)} %param.8) | copy-start | bytes 9220
  341.0 93.7 %all-to-all-start.1 = ((bf16[8,96,2,1280]{3,1,2,0:T(8,128)(2,1)}), bf16[8,96,2,1280]{3,1,2,0:T(8,128)(2,1)}, u32[]{:S(2)}, u32[]{:S(2)}) async-start(bf16[8,96,2,1280]{3,1,2,0:T(8,128)(2,1)} %copy.21), calls=%async_computation.2 | async-start | bytes 7864320 | tf_op jit(solution)/shard_map/all_to_all | solution.py:44
Sparse Core Ops, SparseCore 0:
  149.9 136.7 reduce-scatter.1
  290.9 37.3 all-gather.1
where the time goes:
time: 474 us; the launch traced here: 473 us
  waiting for transfers between devices  262 us (55%)
  blocking collectives  95.1 us (20%)
  local copies, waits for them, and re-layouts  53.9 us (11%)
  matrix products  25.2 us (5%)
  other arithmetic  17.6 us (4%)
  between operations  13.5 us (3%)
  starting transfers between devices  5.69 us (1%)
    reduce_scatter x1, waiting for transfers between devices, local(): lax.psum_scatter(jnp.stack((gate_part, up_part), axis=2), 'dp', scatter_d...  137 us
    all_to_all x1, blocking collectives, local(): lax.all_to_all(buffer, 'blk', split_axis=0, concat_axis=0, tiled=True)  95.1 us
    all_to_all x1, waiting for transfers between devices, local(): lax.all_to_all(outgoing, 'blk', split_axis=0, concat_axis=0, tiled=True)  87.9 us
    all_gather x1, waiting for transfers between devices, local(): lax.all_gather(hidden, 'dp', axis=2, tiled=True)  37.5 us
    dot_general x1, matrix products, local(): jnp.einsum('mef,edf->med', lax.all_gather(hidden, 'dp', axis=2, tiled=Tru...  10.5 us
  transfers between devices with their start and end apart: 3, of which 3 were waited for; matrix products, arithmetic and copies ran while one was open for 0% of the time, Pallas kernels for 0%

commit v1 on v0

v1 whole, which is shorter than its diff:
```python
import jax
import jax.numpy as jnp
from jax import lax
from jax.sharding import PartitionSpec as P


def routing(expert_ids, gate_vals, held_count, capacity):
    first = lax.axis_index("blk") * held_count
    ids = lax.all_gather(expert_ids, "blk", axis=0, tiled=False)
    gates = lax.all_gather(gate_vals, "blk", axis=0, tiled=False)
    mine = first + jnp.arange(held_count, dtype=jnp.int32)
    match = ids[:, None, :, :] == mine[None, :, None, None]
    member = jnp.any(match, axis=3)
    weight = jnp.sum(jnp.where(match, gates[:, None], 0.0), axis=3)
    tok_rows = ids.shape[1]
    earlier = jnp.triu(jnp.ones((tok_rows, tok_rows), jnp.float32), 1)
    position = jnp.einsum(
        "bht,tu->bhu", member.astype(jnp.bfloat16), earlier.astype(jnp.bfloat16),
        preferred_element_type=jnp.float32,
    )
    slots = jnp.arange(capacity, dtype=jnp.int32).astype(jnp.float32)
    hot = member[:, :, None, :] & (position[:, :, None, :] == slots[None, None, :, None])
    return hot.astype(jnp.bfloat16), jnp.where(hot, weight[:, :, None, :], 0.0)


def local(tokens, expert_ids, gate_vals, w_gate, w_up, w_down):
    blk_size = lax.axis_size("blk")
    tok_rows, width_dev = tokens.shape
    top_k = expert_ids.shape[1]
    held_count = w_gate.shape[0]
    capacity = 2 * tok_rows * top_k // (held_count * blk_size)
    hot, weighted = routing(expert_ids, gate_vals, held_count, capacity)
    everyone = lax.all_gather(tokens, "blk", axis=0, tiled=False)
    routed = jnp.einsum("bhpt,btd->hbpd", hot, everyone, preferred_element_type=jnp.float32)
    routed = routed.astype(jnp.bfloat16).reshape(held_count, blk_size * capacity, width_dev)
    gate_part = jnp.einsum("emd,edf->emf", routed, w_gate, preferred_element_type=jnp.float32)
    up_part = jnp.einsum("emd,edf->emf", routed, w_up, preferred_element_type=jnp.float32)
    both = jnp.stack((gate_part, up_part), axis=0)
    summed = lax.psum_scatter(both, "dp", scatter_dimension=2, tiled=True)
    hidden = (jax.nn.silu(summed[0]) * summed[1]).astype(jnp.bfloat16)
    hidden = lax.all_gather(hidden, "dp", axis=1, tiled=True)
    result = jnp.einsum("emf,edf->emd", hidden, w_down, preferred_element_type=jnp.float32)
    result = result.astype(jnp.bfloat16).reshape(held_count, blk_size, capacity, width_dev)
    high = weighted.astype(jnp.bfloat16)
    low = (weighted - high.astype(jnp.float32)).astype(jnp.bfloat16)
    partial = jnp.einsum(
        "bhpt,hbpd->btd", high, result, preferred_element_type=jnp.float32
    ) + jnp.einsum("bhpt,hbpd->btd", low, result, preferred_element_type=jnp.float32)
    partial = partial.astype(jnp.bfloat16).reshape(blk_size * tok_rows, width_dev)
    return lax.psum_scatter(partial, "blk", scatter_dimension=0, tiled=True)


def solution(mesh):
    return jax.shard_map(
        local,
        mesh=mesh,
        in_specs=(
            P("blk", "dp"),
            P("blk", None),
            P("blk", None),
            P("blk", "dp", None),
            P("blk", "dp", None),
            P("blk", "dp", None),
        ),
        out_specs=P("blk", "dp"),
        check_vma=False,
    )
```

time: 474 us -> 364 us (0.77)
  local copies, waits for them, and re-layouts: 53.9 us -> 2.07 us
  blocking collectives: 95.1 us -> 63.6 us
  waiting for transfers between devices: 262 us -> 242 us
  matrix products: 25.2 us -> 32.1 us
  other arithmetic: 17.6 us -> 11 us
  starting transfers between devices: 5.69 us -> 0.12 us
    all_to_all x1 -> x0, blocking collectives: 95.1 us -> none  [local(): lax.all_to_all(buffer, 'blk', split_axis=0, concat_axis=0, tiled=True)]
    all_to_all x1 -> x0, waiting for transfers between devices: 87.9 us -> none  [local(): lax.all_to_all(outgoing, 'blk', split_axis=0, concat_axis=0, tiled=True)]
    reduce_scatter x1 -> x2, waiting for transfers between devices: 137 us -> 208 us  [the longest x1 137 us: local(): summed = lax.psum_scatter(both, 'dp', scatter_dimension=2, tiled=True)]
    all_gather x0 -> x2, blocking collectives: none -> 63.6 us  [the longest x1 32.9 us: routing(): ids = lax.all_gather(expert_ids, 'blk', axis=0, tiled=False)]
    reshape x5 -> x0, local copies, waits for them, and re-layouts: 22.2 us -> none  [the longest x1 9.04 us: local(): lax.all_to_all(outgoing, 'blk', split_axis=0, concat_axis=0, tiled=True)]
    scatter x1 -> x0, local copies, waits for them, and re-layouts: 9.07 us -> none  [local(): buffer = jnp.zeros((blk_size * capacity * held_count, width_dev), jnp.bfl...]
    all_to_all x2 -> x0, local copies, waits for them, and re-layouts: 8.69 us -> none  [the longest x1 8.06 us: local(): lax.all_to_all(outgoing, 'blk', split_axis=0, concat_axis=0, tiled=True)]
    gather x1 -> x0, local copies, waits for them, and re-layouts: 7.02 us -> none  [local(): returned[slot_index].astype(jnp.float32).reshape(tok_rows, top_k, width_dev)]
  transfers between devices with their start and end apart: 3 -> 4, of which waited for: 3 -> 4; matrix products, arithmetic and copies ran while one was open for 0% -> 0% of each run, Pallas kernels for 0% -> 0%
where the time goes in v1:
time: 364 us
  waiting for transfers between devices  242 us (66%)
  blocking collectives  63.6 us (17%)
  matrix products  32.1 us (9%)
  between operations  13.2 us (4%)
  other arithmetic  11 us (3%)
    reduce_scatter x1, waiting for transfers between devices, local(): summed = lax.psum_scatter(both, 'dp', scatter_dimension=2, tiled=True)  137 us
    reduce_scatter x1, waiting for transfers between devices, local(): return lax.psum_scatter(partial, 'blk', scatter_dimension=0, tiled=True)  71.2 us
    all_gather x1, blocking collectives, routing(): ids = lax.all_gather(expert_ids, 'blk', axis=0, tiled=False)  32.9 us
    all_gather x1, blocking collectives, routing(): gates = lax.all_gather(gate_vals, 'blk', axis=0, tiled=False)  30.7 us
    all_gather x1, waiting for transfers between devices, local(): everyone = lax.all_gather(tokens, 'blk', axis=0, tiled=False)  26.3 us
    dot_general x1, matrix products, local(): jnp.einsum('emf,edf->emd', hidden, w_down, preferred_element_type=jnp.flo...  10.5 us
    dot_general x1, matrix products, local(): jnp.einsum('emd,edf->emf', routed, w_gate, preferred_element_type=jnp.flo...  8.55 us
  transfers between devices with their start and end apart: 4, of which 4 were waited for; matrix products, arithmetic and copies ran while one was open for 0% of the time, Pallas kernels for 0%

profile of v1, /device:TPU:0, one launch (start us, length us, event | category | flops | bytes accessed | tf_op | source)
XLA Modules:
  0.0 363.6 jit_solution(16036766468942686623)
XLA Ops:
  6.5 0.0 all-gather.8.cloned.1.call-start
  6.5 0.7 all-gather.8.cloned.1.call-update
  7.3 0.0 reduce-scatter.3.cloned.1.call-start
  7.3 32.9 %all-gather = s32[1024,6]{0,1:T(8,128)S(1)} all-gather(s32[128,6]{0,1:T(8,128)} %param.7), channel_id=2, replica_groups=mesh['blk'=8,'dp'=4] {'blk'}, dimensions={0}, use_global_device_ids=true | all-gather | bytes 27648 | tf_op jit(solution)/shard_map/all_gather | solution.py:9
  40.2 0.1 compare_reduce_fusion
  40.3 0.1 fusion.24
  40.4 26.3 %all-gather.8.cloned.1.call-done = bf16[1024,1280]{1,0:T(8,128)(2,1)} async-done(((bf16[128,1280]{1,0:T(8,128)(2,1)}), bf16[1024,1280]{1,0:T(8,128)(2,1)}) %all-gather.8.cloned.1.call-update) | async-done | bytes 2621456 | tf_op jit(solution)/shard_map/all_gather | solution.py:33
  66.8 0.0 slice-start
  66.8 3.1 fusion.1
  69.9 0.0 slice-start.1
  69.9 0.3 copy.23
  70.2 0.0 slice-done
  70.2 1.7 slice-done.1
  71.9 6.2 %convolution_bitcast_fusion = f32[1,2,768,1536]{3,2,1,0:T(8,128)S(1)} fusion(bf16[2,768,1280]{2,1,0:T(8,128)(2,1)S(1)} %bitcast.58, bf16[2,1280,1536]{2,1,0:T(8,128)(2,1)S(1)} %bitcast.67), kind=kOutput, calls=%fused_computation.1 | convolution fusion | flops 6039797760 | bytes 21233664 | tf_op jit(solution)/shard_map/emd,edf->emf/dot_general | solution.py:37
  78.2 8.5 %convolution_bitcast_fusion.1 = f32[1,2,768,1536]{3,2,1,0:T(8,128)S(1)} fusion(bf16[2,768,1280]{2,1,0:T(8,128)(2,1)S(1)} %bitcast.59, bf16[2,1280,1536]{2,1,0:T(8,128)(2,1)} %param.9), kind=kOutput, calls=%fused_computation.2 | convolution fusion | flops 6039797760 | bytes 21233664 | tf_op jit(solution)/shard_map/emd,edf->emf/dot_general | solution.py:36
  86.7 6.7 %pad_maximum_fusion = f32[2,2,768,1536]{3,2,1,0:T(8,128)} fusion(f32[1,2,768,1536]{3,2,1,0:T(8,128)S(1)} %convolution_bitcast_fusion, f32[1,2,768,1536]{3,2,1,0:T(8,128)S(1)} %convolution_bitcast_fusion.1), kind=kLoop, calls=%fused_computation | loop fusion | flops 4718592 | bytes 37748736 | tf_op jit(solution)/shard_map/stack | solution.py:38
  93.4 0.0 reduce-scatter.3.cloned.1.call-update
  93.5 0.0 copy-start
  93.5 0.0 all-gather.6.cloned.1.call-start
  93.5 136.5 %reduce-scatter.3.cloned.1.call-done = f32[2,2,192,1536]{3,2,1,0:T(8,128)} async-done(((f32[2,2,768,1536]{3,2,1,0:T(8,128)}), f32[2,2,192,1536]{3,2,1,0:T(8,128)}) %reduce-scatter.3.cloned.1.call-update) | async-done | bytes 4718608 | tf_op jit(solution)/shard_map/reduce_scatter | solution.py:39
  230.0 4.1 %fusion.6 = bf16[2,192,1536]{2,1,0:T(8,128)(2,1)} fusion(f32[2,2,192,1536]{3,2,1,0:T(8,128)} %reduce-scatter.3.cloned.1.call-done), kind=kLoop, calls=%fused_computation.13 | loop fusion | flops 3538944 | bytes 5898240 | tf_op jit(solution)/shard_map/convert_element_type | solution.py:40
  234.2 0.0 all-gather.6.cloned.1.call-update
  234.2 0.0 reduce-scatter.5.cloned.1.call-start
  234.2 0.0 copy-done
  234.3 30.7 %all-gather.1 = f32[1024,6]{0,1:T(8,128)S(1)} all-gather(f32[128,6]{0,1:T(8,128)S(1)} %copy-done), channel_id=3, replica_groups=mesh['blk'=8,'dp'=4] {'blk'}, dimensions={0}, use_global_device_ids=true | all-gather | bytes 27648 | tf_op jit(solution)/shard_map/all_gather | solution.py:10
  264.9 0.1 fusion.22
  265.0 6.7 %all-gather.6.cloned.1.call-done = bf16[2,768,1536]{2,1,0:T(8,128)(2,1)} async-done(((bf16[2,192,1536]{2,1,0:T(8,128)(2,1)}), bf16[2,768,1536]{2,1,0:T(8,128)(2,1)}) %all-gather.6.cloned.1.call-update) | async-done | bytes 4718608 | tf_op jit(solution)/shard_map/all_gather | solution.py:41
  271.8 10.5 %convolution_convert_fusion = bf16[2,768,1280]{2,1,0:T(8,128)(2,1)S(1)} fusion(bf16[2,768,1536]{2,1,0:T(8,128)(2,1)} %all-gather.6.cloned.1.call-done, bf16[2,1280,1536]{2,1,0:T(8,128)(2,1)} %param.11), kind=kOutput, calls=%fused_computation.5 | convolution fusion | flops 6041763840 | bytes 16515072 | tf_op jit(solution)/shard_map/emf,edf->emd/dot_general | solution.py:42
  282.2 1.0 fusion.3
  283.2 2.6 fusion
  285.9 0.0 reduce-scatter.5.cloned.1.call-update
  285.9 71.2 %reduce-scatter.5.cloned.1.call-done = bf16[128,1280]{1,0:T(8,128)(2,1)} async-done(((bf16[1024,1280]{1,0:T(8,128)(2,1)}), bf16[128,1280]{1,0:T(8,128)(2,1)}) %reduce-scatter.5.cloned.1.call-update) | async-done | bytes 327696 | tf_op jit(solution)/shard_map/reduce_scatter | solution.py:50
  (8 shorter events, 0.0 us)
Async XLA Ops:
  6.5 60.2 %all-gather.8.cloned.1.call-start = ((), (), s32[]{:S(2)}) async-start(), calls=%async_computation.5 | async-start | bytes 2949120 | tf_op jit(solution)/shard_map/all_gather | solution.py:33
  7.3 222.8 %reduce-scatter.3.cloned.1.call-start = ((), (), s32[]{:S(2)}) async-start(), calls=%async_computation.2 | async-start | bytes 23592960 | tf_op jit(solution)/shard_map/reduce_scatter | solution.py:39
  66.8 3.4 slice-start
  69.9 2.0 slice-start.1
  93.5 140.8 %copy-start = (f32[128,6]{0,1:T(8,128)S(1)}, f32[128,6]{0,1:T(8,128)}, u32[]{:S(2)}) copy-start(f32[128,6]{0,1:T(8,128)} %param.8) | copy-start | bytes 9220
  93.5 178.3 %all-gather.6.cloned.1.call-start = ((), (), s32[]{:S(2)}) async-start(), calls=%async_computation.3 | async-start | bytes 5898240 | tf_op jit(solution)/shard_map/all_gather | solution.py:41
  234.2 122.9 %reduce-scatter.5.cloned.1.call-start = ((), (), s32[]{:S(2)}) async-start(), calls=%async_computation.4 | async-start | bytes 2949120 | tf_op jit(solution)/shard_map/reduce_scatter | solution.py:50
Sparse Core Ops, SparseCore 0:
  9.5 57.1 all-gather.7
  93.6 136.4 reduce-scatter.2
  234.3 37.4 all-gather.5
  286.0 71.0 reduce-scatter.4

commit v2 on v1

--- a/solution.py
+++ b/solution.py
@@ -1,13 +1,260 @@
+import functools
+
 import jax
 import jax.numpy as jnp
 from jax import lax
+from jax.experimental import pallas as pl
+from jax.experimental.pallas import tpu as pltpu
 from jax.sharding import PartitionSpec as P
+
+MESH = pl.DeviceIdType.MESH
+VMEM_BYTES = 66_000_000
+
+
+def flip(a, m, size):
+    total, unit = 0, 1
+    while unit < size:
+        total = total + lax.rem(lax.div(a, unit) + lax.div(m, unit), 2) * unit
+        unit *= 2
+    return total
+
+
+def fused_kernel(
+    n_blk, tok_ref, hot_ref, high_ref, low_ref, wg_hbm, wu_hbm, wd_hbm, out_ref,
+    wg, wu, wd, everyone, routed, part, near, far_out, far_in, hidden, rows_out,
+    outgoing, arrived, acc,
+    w_sem, tok_s, tok_r, near_s, near_r, far_s, far_r, hy_s, hy_r, hc_s, hc_r, hf_s, hf_r, ret_s, ret_r,
+):
+    blk = lax.axis_index("blk")
+    dp = lax.axis_index("dp")
+    y, c = lax.div(dp, 2), lax.rem(dp, 2)
+    mate = (blk, y * 2 + (1 - c))
+    across = (blk, (1 - y) * 2 + c)
+    ff = wg.shape[2]
+    width = wg.shape[1]
+    half = part.shape[3]
+    cap = 2 * half
+
+    def copy(src, dst, send, recv, device):
+        return pltpu.make_async_remote_copy(
+            src_ref=src, dst_ref=dst, send_sem=send, recv_sem=recv,
+            device_id=device, device_id_type=MESH,
+        )
+
+    def peer(m):
+        return (flip(blk, m, n_blk), dp)
+
+    def mask_of(i):
+        m = jnp.where(i == 0, 0, jnp.where(i == 1, 2, i + 2))
+        return jnp.where(i == n_blk - 2, 3, jnp.where(i == n_blk - 1, 1, m))
+
+    def tok_direct(m):
+        return copy(tok_ref, everyone.at[m], tok_s.at[m], tok_r.at[m], peer(m))
+
+    def tok_onward(m):
+        return copy(everyone.at[m], everyone.at[m + 1], tok_s.at[m + 1], tok_r.at[m + 1], peer(1))
+
+    def near_copy(j):
+        return copy(part.at[lax.rem(j, 2), 1 - c], near.at[j], near_s.at[j], near_r.at[j], mate)
+
+    def far_copy(j):
+        return copy(far_out.at[j], far_in.at[j], far_s.at[j], far_r.at[j], across)
+
+    def hidden_far(j):
+        return copy(hidden.at[j, y, c], hidden.at[j, y, c], hy_s.at[j], hy_r.at[j], across)
+
+    def hidden_near(j):
+        return copy(hidden.at[j, y, c], hidden.at[j, y, c], hc_s.at[j], hc_r.at[j], mate)
+
+    def hidden_onward(j):
+        return copy(hidden.at[j, 1 - y, c], hidden.at[j, 1 - y, c], hf_s.at[j], hf_r.at[j], mate)
+
+    def ret_copy(m):
+        return copy(outgoing.at[m], arrived.at[m], ret_s.at[m], ret_r.at[m], peer(m))
+
+    loads = [
+        pltpu.make_async_copy(wg_hbm, wg, w_sem.at[0]),
+        pltpu.make_async_copy(wu_hbm, wu, w_sem.at[1]),
+        pltpu.make_async_copy(wd_hbm, wd, w_sem.at[2]),
+    ]
+    for load in loads:
+        load.start()
+
+    barrier = pltpu.get_barrier_semaphore()
+    for m in range(1, n_blk):
+        pl.semaphore_signal(barrier, inc=1, device_id=peer(m), device_id_type=MESH)
+    for device in (mate, across):
+        pl.semaphore_signal(barrier, inc=1, device_id=device, device_id_type=MESH)
+    pl.semaphore_wait(barrier, n_blk + 1)
+
+    for m in [1] + list(range(2, n_blk, 2)):
+        tok_direct(m).start()
+    everyone[0] = tok_ref[...]
+
+    def project(i):
+        m = mask_of(i)
+
+        @pl.when(i > 0)
+        def _():
+            tok_direct(m).wait_recv()
+
+        @pl.when((m > 0) & (lax.rem(m, 2) == 0))
+        def _():
+            tok_onward(m).start()
+
+        routed[...] = jnp.dot(
+            hot_ref[flip(blk, m, n_blk)], everyone[m], preferred_element_type=jnp.float32
+        ).astype(jnp.bfloat16)
+
+        @pl.when(i == 0)
+        def _():
+            loads[0].wait()
+            loads[1].wait()
+
+        slot = lax.rem(i, 2)
+        tile = ff // 3 if ff % 384 == 0 else ff
+        for h in range(2):
+            rows = routed[h * cap:(h + 1) * cap, :]
+            for which, w in enumerate((wg, wu)):
+                for f in range(0, ff, tile):
+                    got = jnp.dot(rows, w[h, :, f:f + tile], preferred_element_type=jnp.float32)
+                    at = which * ff + f
+                    part[slot, 0, h, :, at:at + tile] = got[:half]
+                    part[slot, 1, h, :, at:at + tile] = got[half:]
+        near_copy(i).start()
+
+    def join(j):
+        near_copy(j).wait()
+        slot = lax.rem(j, 2)
+        far_out[j] = (part[slot, c, 1 - y] + near[j, 1 - y]).astype(jnp.bfloat16)
+        far_copy(j).start()
+        near[j, y] = near[j, y] + part[slot, c, y]
+
+    def activate(j):
+        far_copy(j).wait_recv()
+        gate = near[j, y, :, :ff] + far_in[j, :, :ff].astype(jnp.float32)
+        up = near[j, y, :, ff:] + far_in[j, :, ff:].astype(jnp.float32)
+        hidden[j, y, c] = (gate / (1.0 + jnp.exp(-gate)) * up).astype(jnp.bfloat16)
+        hidden_far(j).start()
+        hidden_near(j).start()
+
+    def relay(j):
+        hidden_far(j).wait_recv()
+        hidden_onward(j).start()
+
+    def finish(j):
+        @pl.when(j == 0)
+        def _():
+            loads[2].wait()
+
+        hidden_near(j).wait_recv()
+        hidden_onward(j).wait_recv()
+        m = mask_of(j)
+        tile = 256 if width % 256 == 0 else width
+        for h in range(2):
+            rows = hidden[j, h].reshape(cap, ff)
+            for d in range(0, width, tile):
+                rows_out[h * cap:(h + 1) * cap, d:d + tile] = lax.dot_general(
+                    rows, wd[h, d:d + tile, :], (((1,), (1,)), ((), ())),
+                    preferred_element_type=jnp.float32,
+                ).astype(jnp.bfloat16)
+        target = flip(blk, m, n_blk)
+        mixed = jnp.dot(high_ref[target], rows_out[...], preferred_element_type=jnp.float32)
+        mixed = mixed + jnp.dot(low_ref[target], rows_out[...], preferred_element_type=jnp.float32)
+
+        @pl.when(m == 0)
+        def _():
+            acc[...] = mixed
+
+        @pl.when(m > 0)
+        def _():
+            outgoing[m] = mixed.astype(jnp.bfloat16)
+            ret_copy(m).start()
+
+    stages = (project, join, activate, relay, finish)
+
+    def step(i, carry):
+        for lag, stage in enumerate(stages):
+            @pl.when((i >= lag) & (i - lag < n_blk))
+            def _():
+                stage(i - lag)
+        return carry
+
+    lax.fori_loop(0, n_blk + len(stages) - 1, step, 0)
+
+    def gather_in(m, carry):
+        ret_copy(m).wait_recv()
+        acc[...] += arrived[m].astype(jnp.float32)
+        return carry
+
+    lax.fori_loop(1, n_blk, gather_in, 0)
+    out_ref[...] = acc[...].astype(jnp.bfloat16)
+
+    def drain(m, carry):
+        far_copy(m).wait_send()
+        hidden_far(m).wait_send()
+        hidden_near(m).wait_send()
+        hidden_onward(m).wait_send()
+
+        @pl.when(m > 0)
+        def _():
+            tok_direct(m).wait_send()
+            ret_copy(m).wait_send()
+
+        return carry
+
+    lax.fori_loop(0, n_blk, drain, 0)
+
+
+def fused(tokens, expert_ids, gate_vals, w_gate, w_up, w_down):
+    n_blk = lax.axis_size("blk")
+    tok_rows, width = tokens.shape
+    held, _, ff = w_gate.shape
+    capacity = 2 * tok_rows * expert_ids.shape[1] // (held * n_blk)
+    slots, half = held * capacity, capacity // 2
+    hot, weighted = routing(expert_ids, gate_vals, held, capacity)
+    hot = hot.reshape(n_blk, slots, tok_rows)
+    weighted = weighted.reshape(n_blk, slots, tok_rows).transpose(0, 2, 1)
+    high = weighted.astype(jnp.bfloat16)
+    low = (weighted - high.astype(jnp.float32)).astype(jnp.bfloat16)
+    bf, f32 = jnp.bfloat16, jnp.float32
+    sems = [pltpu.SemaphoreType.DMA((n_blk,)) for _ in range(14)]
+    vmem = pl.BlockSpec(memory_space=pltpu.VMEM)
+    anywhere = pl.BlockSpec(memory_space=pl.ANY)
+    return pl.pallas_call(
+        functools.partial(fused_kernel, n_blk),
+        out_shape=jax.ShapeDtypeStruct((tok_rows, width), bf),
+        in_specs=[vmem] * 4 + [anywhere] * 3,
+        out_specs=vmem,
+        scratch_shapes=[
+            pltpu.VMEM(w_gate.shape, bf),
+            pltpu.VMEM(w_up.shape, bf),
+            pltpu.VMEM(w_down.shape, bf),
+            pltpu.VMEM((n_blk, tok_rows, width), bf),
+            pltpu.VMEM((slots, width), bf),
+            pltpu.VMEM((2, 2, held, half, 2 * ff), f32),
+            pltpu.VMEM((n_blk, held, half, 2 * ff), f32),
+            pltpu.VMEM((n_blk, half, 2 * ff), bf),
+            pltpu.VMEM((n_blk, half, 2 * ff), bf),
+            pltpu.VMEM((n_blk, held, 2, half, ff), bf),
+            pltpu.VMEM((slots, width), bf),
+            pltpu.VMEM((n_blk, tok_rows, width), bf),
+            pltpu.VMEM((n_blk, tok_rows, width), bf),
+            pltpu.VMEM((tok_rows, width), f32),
+            pltpu.SemaphoreType.DMA((3,)),
+        ] + sems,
+        compiler_params=pltpu.CompilerParams(
+            collective_id=0, has_side_effects=True, vmem_limit_bytes=VMEM_BYTES
+        ),
+    )(tokens, hot, high, low, w_gate, w_up, w_down)
 
 
 def routing(expert_ids, gate_vals, held_count, capacity):
     first = lax.axis_index("blk") * held_count
-    ids = lax.all_gather(expert_ids, "blk", axis=0, tiled=False)
-    gates = lax.all_gather(gate_vals, "blk", axis=0, tiled=False)
+    top_k = expert_ids.shape[1]
+    both = jnp.concatenate((expert_ids.astype(jnp.float32), gate_vals), axis=1)
+    both = lax.all_gather(both, "blk", axis=0, tiled=False)
+    ids, gates = both[:, :, :top_k].astype(jnp.int32), both[:, :, top_k:]
     mine = first + jnp.arange(held_count, dtype=jnp.int32)
     match = ids[:, None, :, :] == mine[None, :, None, None]
     member = jnp.any(match, axis=3)
@@ -50,9 +297,17 @@
     return lax.psum_scatter(partial, "blk", scatter_dimension=0, tiled=True)
 
 
+def choose(tokens, expert_ids, gate_vals, w_gate, w_up, w_down):
+    n_blk, held = lax.axis_size("blk"), w_gate.shape[0]
+    capacity = 2 * tokens.shape[0] * expert_ids.shape[1] // (held * n_blk)
+    fits = lax.axis_size("dp") == 4 and held == 2 and n_blk == 8 and capacity % 32 == 0
+    body = fused if fits else local
+    return body(tokens, expert_ids, gate_vals, w_gate, w_up, w_down)
+
+
 def solution(mesh):
     return jax.shard_map(
-        local,
+        choose,
         mesh=mesh,
         in_specs=(
             P("blk", "dp"),

time: 364 us -> 165 us (0.45)
  waiting for transfers between devices: 242 us -> 0 us
  Pallas kernels: 0 us -> 125 us
  matrix products: 32.1 us -> 0.13 us
  blocking collectives: 63.6 us -> 32.3 us
  between operations: 13.2 us -> 0.11 us
  other arithmetic: 11 us -> 3.78 us
    reduce_scatter x2 -> x0, waiting for transfers between devices: 208 us -> none  [the longest x1 137 us: local(): summed = lax.psum_scatter(both, 'dp', scatter_dimension=2, tiled=True)]
    pallas_call x0 -> x1, Pallas kernels: none -> 125 us  [fused(): pl.pallas_call(functools.partial(fused_kernel, n_blk), out_shape=jax.Shap...]
    all_gather x2 -> x0, waiting for transfers between devices: 33.1 us -> none  [the longest x1 26.3 us: local(): everyone = lax.all_gather(tokens, 'blk', axis=0, tiled=False)]
    dot_general x6 -> x0, matrix products: 32 us -> none  [the longest x1 10.5 us: local(): jnp.einsum('emf,edf->emd', hidden, w_down, preferred_element_type=jnp.flo...]
    all_gather x2 -> x1, blocking collectives: 63.6 us -> 32.3 us  [routing(): both = lax.all_gather(both, 'blk', axis=0, tiled=False)]
    another operation x1 -> x0, other arithmetic: 6.72 us -> none  [local(): both = jnp.stack((gate_part, up_part), axis=0)]
  transfers between devices with their start and end apart: 4 -> 0, of which waited for: 4 -> 0; matrix products, arithmetic and copies ran while one was open for 0% -> 0% of each run, Pallas kernels for 0% -> 0%
where the time goes in v2:
time: 165 us
  Pallas kernels  125 us (76%)
  blocking collectives  32.3 us (20%)
  local copies, waits for them, and re-layouts  4.07 us (2%)
  other arithmetic  3.78 us (2%)
    pallas_call x1, Pallas kernels, fused(): pl.pallas_call(functools.partial(fused_kernel, n_blk), out_shape=jax.Shap...  125 us
    all_gather x1, blocking collectives, routing(): both = lax.all_gather(both, 'blk', axis=0, tiled=False)  32.3 us

profile of v2, /device:TPU:0, one launch (start us, length us, event | category | flops | bytes accessed | tf_op | source)
XLA Modules:
  0.0 165.2 jit_solution(7206480632007100317)
XLA Ops:
  0.0 0.7 convert_element_type.30
  0.7 0.7 pad_maximum_fusion
  1.4 32.3 %all-gather = f32[1024,12]{0,1:T(8,128)S(1)} all-gather(f32[128,12]{0,1:T(8,128)S(1)} %pad_maximum_fusion), channel_id=2, replica_groups=mesh['blk'=8,'dp'=4] {'blk'}, dimensions={0}, use_global_device_ids=true | all-gather | bytes 55296 | tf_op jit(solution)/shard_map/all_gather | solution.py:256
  33.8 0.1 fusion.1
  33.9 0.1 broadcast_in_dim.44
  33.9 0.3 copy.25
  34.3 0.1 compare_reduce_fusion
  34.3 0.1 fusion.3
  34.5 0.1 eq.37
  34.6 0.3 copy.22
  34.9 0.1 and.13
  35.0 0.4 copy.23
  35.4 0.1 eq.40
  35.5 1.1 fusion
  36.7 1.0 bitcast_convert_fusion.high_ref
  37.7 0.1 convert_element_type.34
  37.8 1.0 copy.26.hot_ref
  38.7 124.8 %shard_map.64 = bf16[128,1280]{1,0:T(8,128)(2,1)} custom-call(bf16[128,1280]{1,0:T(8,128)(2,1)} %tok_ref.1, bf16[8,192,128]{2,1,0:T(8,128)(2,1)} %copy.26.hot_ref, bf16[8,128,192]{2,1,0:T(8,128)(2,1)} %bitcast_convert_fusion.high_ref, bf16[8,128,192]{2,1,0:T(8,128)(2,1)} %get-tuple-element.5.low_ref, bf16[2,1280,1536]{2,1,0:T(8,128)(2,1)} %wg_hbm.1, ...), custom_call_target="tpu_custom_call" | custom-call | tf_op jit(solution)/shard_map/pallas_call | solution.py:224
  163.5 1.7 %copy.29 = bf16[128,1280]{1,0:T(8,128)(2,1)} copy(bf16[128,1280]{1,0:T(8,128)(2,1)} %shard_map.64) | data formatting | bytes 655360
  (9 shorter events, 0.1 us)

commit v3 on v2

--- a/solution.py
+++ b/solution.py
@@ -20,10 +20,10 @@
 
 
 def fused_kernel(
-    n_blk, tok_ref, hot_ref, high_ref, low_ref, wg_hbm, wu_hbm, wd_hbm, out_ref,
+    n_blk, tok_ref, info_ref, wg_hbm, wu_hbm, wd_hbm, out_ref,
     wg, wu, wd, everyone, routed, part, near, far_out, far_in, hidden, rows_out,
-    outgoing, arrived, acc,
-    w_sem, tok_s, tok_r, near_s, near_r, far_s, far_r, hy_s, hy_r, hc_s, hc_r, hf_s, hf_r, ret_s, ret_r,
+    outgoing, arrived, acc, info, high, low, hot,
+    w_sem, tok_s, tok_r, near_s, near_r, far_s, far_r, hy_s, hy_r, hc_s, hc_r, hf_s, hf_r, ret_s, ret_r, info_s, info_r,
 ):
     blk = lax.axis_index("blk")
     dp = lax.axis_index("dp")
@@ -51,6 +51,9 @@
     def tok_direct(m):
         return copy(tok_ref, everyone.at[m], tok_s.at[m], tok_r.at[m], peer(m))
 
+    def info_direct(m):
+        return copy(info_ref, info.at[m], info_s.at[m], info_r.at[m], peer(m))
+
     def tok_onward(m):
         return copy(everyone.at[m], everyone.at[m + 1], tok_s.at[m + 1], tok_r.at[m + 1], peer(1))
 
@@ -87,23 +90,50 @@
         pl.semaphore_signal(barrier, inc=1, device_id=device, device_id_type=MESH)
     pl.semaphore_wait(barrier, n_blk + 1)
 
+    for m in range(1, n_blk):
+        info_direct(m).start()
     for m in [1] + list(range(2, n_blk, 2)):
         tok_direct(m).start()
     everyone[0] = tok_ref[...]
+    info[0] = info_ref[...]
+    tok_rows = tok_ref.shape[0]
+    lines = info_ref.shape[0] // 2
+
+    def slots_of(m):
+        square = (tok_rows, tok_rows)
+        before = lax.broadcasted_iota(jnp.int32, square, 0) < lax.broadcasted_iota(jnp.int32, square, 1)
+        before = jnp.where(before, 1.0, 0.0).astype(jnp.bfloat16)
+        slot = lax.broadcasted_iota(jnp.int32, (cap, tok_rows), 0).astype(jnp.float32)
+        ids, gates = info[m, :lines], info[m, lines:]
+        for h in range(2):
+            match = ids == (2 * blk + h).astype(jnp.float32)
+            member = jnp.sum(jnp.where(match, 1.0, 0.0), axis=0, keepdims=True)
+            weight = jnp.sum(jnp.where(match, gates, 0.0), axis=0, keepdims=True)
+            wide = jnp.broadcast_to(member, (16, tok_rows)).astype(jnp.bfloat16)
+            position = jnp.dot(wide, before, preferred_element_type=jnp.float32)[0:1]
+            taken = (slot == position) & (member > 0.5)
+            weighted = jnp.where(taken, weight, 0.0)
+            top = weighted.astype(jnp.bfloat16)
+            span = slice(h * cap, (h + 1) * cap)
+            high[m, span, :] = top
+            low[m, span, :] = (weighted - top.astype(jnp.float32)).astype(jnp.bfloat16)
+            hot[span, :] = jnp.where(taken, 1.0, 0.0).astype(jnp.bfloat16)
 
     def project(i):
         m = mask_of(i)
 
         @pl.when(i > 0)
         def _():
+            info_direct(m).wait_recv()
             tok_direct(m).wait_recv()
 
         @pl.when((m > 0) & (lax.rem(m, 2) == 0))
         def _():
             tok_onward(m).start()
 
+        slots_of(m)
         routed[...] = jnp.dot(
-            hot_ref[flip(blk, m, n_blk)], everyone[m], preferred_element_type=jnp.float32
+            hot[...], everyone[m], preferred_element_type=jnp.float32
         ).astype(jnp.bfloat16)
 
         @pl.when(i == 0)
@@ -158,9 +188,11 @@
                     rows, wd[h, d:d + tile, :], (((1,), (1,)), ((), ())),
                     preferred_element_type=jnp.float32,
                 ).astype(jnp.bfloat16)
-        target = flip(blk, m, n_blk)
-        mixed = jnp.dot(high_ref[target], rows_out[...], preferred_element_type=jnp.float32)
-        mixed = mixed + jnp.dot(low_ref[target], rows_out[...], preferred_element_type=jnp.float32)
+        over_slots = (((0,), (0,)), ((), ()))
+        mixed = lax.dot_general(high[m], rows_out[...], over_slots, preferred_element_type=jnp.float32)
+        mixed = mixed + lax.dot_general(
+            low[m], rows_out[...], over_slots, preferred_element_type=jnp.float32
+        )
 
         @pl.when(m == 0)
         def _():
@@ -171,10 +203,10 @@
             outgoing[m] = mixed.astype(jnp.bfloat16)
             ret_copy(m).start()
 
-    stages = (project, join, activate, relay, finish)
+    stages = ((1, join), (2, activate), (0, project), (3, relay), (4, finish))
 
     def step(i, carry):
-        for lag, stage in enumerate(stages):
+        for lag, stage in stages:
             @pl.when((i >= lag) & (i - lag < n_blk))
             def _():
                 stage(i - lag)
@@ -198,6 +230,7 @@
 
         @pl.when(m > 0)
         def _():
+            info_direct(m).wait_send()
             tok_direct(m).wait_send()
             ret_copy(m).wait_send()
 
@@ -212,19 +245,18 @@
     held, _, ff = w_gate.shape
     capacity = 2 * tok_rows * expert_ids.shape[1] // (held * n_blk)
     slots, half = held * capacity, capacity // 2
-    hot, weighted = routing(expert_ids, gate_vals, held, capacity)
-    hot = hot.reshape(n_blk, slots, tok_rows)
-    weighted = weighted.reshape(n_blk, slots, tok_rows).transpose(0, 2, 1)
-    high = weighted.astype(jnp.bfloat16)
-    low = (weighted - high.astype(jnp.float32)).astype(jnp.bfloat16)
+    top_k = expert_ids.shape[1]
+    spare = ((0, -top_k % 8), (0, 0))
+    ids = jnp.pad(expert_ids.T.astype(jnp.float32), spare, constant_values=-1.0)
+    packed = jnp.concatenate((ids, jnp.pad(gate_vals.T, spare)), axis=0)
     bf, f32 = jnp.bfloat16, jnp.float32
-    sems = [pltpu.SemaphoreType.DMA((n_blk,)) for _ in range(14)]
+    sems = [pltpu.SemaphoreType.DMA((n_blk,)) for _ in range(16)]
     vmem = pl.BlockSpec(memory_space=pltpu.VMEM)
     anywhere = pl.BlockSpec(memory_space=pl.ANY)
     return pl.pallas_call(
         functools.partial(fused_kernel, n_blk),
         out_shape=jax.ShapeDtypeStruct((tok_rows, width), bf),
-        in_specs=[vmem] * 4 + [anywhere] * 3,
+        in_specs=[vmem] * 2 + [anywhere] * 3,
         out_specs=vmem,
         scratch_shapes=[
             pltpu.VMEM(w_gate.shape, bf),
@@ -241,12 +273,16 @@
             pltpu.VMEM((n_blk, tok_rows, width), bf),
             pltpu.VMEM((n_blk, tok_rows, width), bf),
             pltpu.VMEM((tok_rows, width), f32),
+            pltpu.VMEM((n_blk,) + packed.shape, f32),
+            pltpu.VMEM((n_blk, slots, tok_rows), bf),
+            pltpu.VMEM((n_blk, slots, tok_rows), bf),
+            pltpu.VMEM((slots, tok_rows), bf),
             pltpu.SemaphoreType.DMA((3,)),
         ] + sems,
         compiler_params=pltpu.CompilerParams(
             collective_id=0, has_side_effects=True, vmem_limit_bytes=VMEM_BYTES
         ),
-    )(tokens, hot, high, low, w_gate, w_up, w_down)
+    )(tokens, packed, w_gate, w_up, w_down)
 
 
 def routing(expert_ids, gate_vals, held_count, capacity):

time: 165 us -> 130 us (0.79)
  blocking collectives: 32.3 us -> 0 us
  local copies, waits for them, and re-layouts: 4.07 us -> 1.72 us
  other arithmetic: 3.78 us -> 1.98 us
    all_gather x1 -> x0, blocking collectives: 32.3 us -> none  [routing(): both = lax.all_gather(both, 'blk', axis=0, tiled=False)]
    convert_element_type x6 -> x1, other arithmetic: 2.92 us -> 0.69 us  [fused(): ids = jnp.pad(expert_ids.T.astype(jnp.float32), spare, constant_values=-1.0)]
where the time goes in v3:
time: 130 us
  Pallas kernels  126 us (97%)
  other arithmetic  1.98 us (2%)
  local copies, waits for them, and re-layouts  1.72 us (1%)
    pallas_call x1, Pallas kernels, fused(): pl.pallas_call(functools.partial(fused_kernel, n_blk), out_shape=jax.Shap...  126 us

profile of v3, /device:TPU:0, one launch (start us, length us, event | category | flops | bytes accessed | tf_op | source)
XLA Modules:
  0.0 129.6 jit_solution(12972934163855700128)
XLA Ops:
  0.0 0.7 convert_bitcast_fusion
  0.7 1.3 select_maximum_fusion.info_ref
  2.0 125.9 %shard_map.64 = bf16[128,1280]{1,0:T(8,128)(2,1)} custom-call(bf16[128,1280]{1,0:T(8,128)(2,1)} %tok_ref.1, f32[16,128]{1,0:T(8,128)} %select_maximum_fusion.info_ref, bf16[2,1280,1536]{2,1,0:T(8,128)(2,1)} %wg_hbm.1, bf16[2,1280,1536]{2,1,0:T(8,128)(2,1)} %wu_hbm.1, bf16[2,1280,1536]{2,1,0:T(8,128)(2,1)} %wd_hbm.1), custom_call_target="tpu_custom_call" | custom-call | tf_op jit(solution)/shard_map/pallas_call | solution.py:256
  127.9 1.7 %copy.8 = bf16[128,1280]{1,0:T(8,128)(2,1)} copy(bf16[128,1280]{1,0:T(8,128)(2,1)} %shard_map.64) | data formatting | bytes 655360

commit v4 on v3

--- a/solution.py
+++ b/solution.py
@@ -80,8 +80,8 @@
         pltpu.make_async_copy(wu_hbm, wu, w_sem.at[1]),
         pltpu.make_async_copy(wd_hbm, wd, w_sem.at[2]),
     ]
-    for load in loads:
-        load.start()
+    loads[0].start()
+    loads[1].start()
 
     barrier = pltpu.get_barrier_semaphore()
     for m in range(1, n_blk):
@@ -136,16 +136,17 @@
             hot[...], everyone[m], preferred_element_type=jnp.float32
         ).astype(jnp.bfloat16)
 
-        @pl.when(i == 0)
-        def _():
-            loads[0].wait()
-            loads[1].wait()
-
         slot = lax.rem(i, 2)
         tile = ff // 3 if ff % 384 == 0 else ff
-        for h in range(2):
-            rows = routed[h * cap:(h + 1) * cap, :]
-            for which, w in enumerate((wg, wu)):
+        for which, w in enumerate((wg, wu)):
+            @pl.when(i == 0)
+            def _():
+                loads[which].wait()
+                if which == 1:
+                    loads[2].start()
+
+            for h in range(2):
+                rows = routed[h * cap:(h + 1) * cap, :]
                 for f in range(0, ff, tile):
                     got = jnp.dot(rows, w[h, :, f:f + tile], preferred_element_type=jnp.float32)
                     at = which * ff + f

time: 130 us -> 130 us (level)
  no operation moved by 1% of the time
where the time goes in v4:
time: 130 us
  Pallas kernels  126 us (97%)
  other arithmetic  1.98 us (2%)
  local copies, waits for them, and re-layouts  1.72 us (1%)
    pallas_call x1, Pallas kernels, fused(): pl.pallas_call(functools.partial(fused_kernel, n_blk), out_shape=jax.Shap...  126 us

profile of v4, /device:TPU:0, one launch (start us, length us, event | category | flops | bytes accessed | tf_op | source)
XLA Modules:
  0.0 129.9 jit_solution(18377866349131734295)
XLA Ops:
  0.0 0.7 convert_bitcast_fusion
  0.7 1.3 select_maximum_fusion.info_ref
  2.0 126.2 %shard_map.64 = bf16[128,1280]{1,0:T(8,128)(2,1)} custom-call(bf16[128,1280]{1,0:T(8,128)(2,1)} %tok_ref.1, f32[16,128]{1,0:T(8,128)} %select_maximum_fusion.info_ref, bf16[2,1280,1536]{2,1,0:T(8,128)(2,1)} %wg_hbm.1, bf16[2,1280,1536]{2,1,0:T(8,128)(2,1)} %wu_hbm.1, bf16[2,1280,1536]{2,1,0:T(8,128)(2,1)} %wd_hbm.1), custom_call_target="tpu_custom_call" | custom-call | tf_op jit(solution)/shard_map/pallas_call | solution.py:257
  128.2 1.7 %copy.8 = bf16[128,1280]{1,0:T(8,128)(2,1)} copy(bf16[128,1280]{1,0:T(8,128)(2,1)} %shard_map.64) | data formatting | bytes 655360
